TPU v7x, 32 devices: a whole 2x2x4 slice. The times are simulated.
32 devices in a mesh: crop: 1, dap: 32 (over z, y, x, core).
Axes of the slice: x: 2, y: 2, z: 4, core: 2. Of those that a mesh axis runs over, the one named last changes fastest.
Arguments:
- homolog_features: bfloat16 [128, 128, 256], P(('crop', 'dap')), may hold values from -6 to 6
- twofold_features: bfloat16 [128, 128, 128], P(('crop', 'dap')), may hold values from -6 to 6
- twofold_offset_map: bfloat16 [128, 8], replicated, may hold values from -0.5 to 0.5
- horizontal_attend_entry_maps: bfloat16 [256, 1024], replicated, may hold values from -2 to 2
- horizontal_attend_exit_map: bfloat16 [256, 256], replicated, may hold values from -0.375 to 0.375
- vertical_attend_entry_maps: bfloat16 [256, 1024], replicated, may hold values from -2 to 2
- vertical_attend_exit_map: bfloat16 [256, 256], replicated, may hold values from -0.375 to 0.375
- tensor_product_factors: bfloat16 [256, 64], replicated, may hold values from -0.375 to 0.375
- tensor_product_exit_map: bfloat16 [1024, 128], replicated, may hold values from -1 to 1
Outputs:
- alignment_output: bfloat16 [128, 128, 256], P('crop', 'dap')
- pair_output: bfloat16 [128, 128, 128], P(('crop', 'dap'))
All inputs are finite; a program needn't handle non-finite values.
Results may differ from a plain program's by a relative error of at most 0.0085.
Values may be sent and summed in bfloat16 or wider, within the bound.
No kernel may reach another device: no remote copies, remote signals or barrier semaphores. Data moves between devices by JAX's collectives and lax.ppermute only.
A program may use at most 64 MiB of HBM per device.

v0:
```python
import math
import jax
import jax.numpy as jnp
from jax import lax
from jax.sharding import PartitionSpec as P

EPSILON = 1e-05


def standardize_features(values):
    values = values.astype(jnp.float32)
    center = values - jnp.mean(values, axis=-1, keepdims=True)
    spread = jnp.mean(center * center, axis=-1, keepdims=True)
    return center * lax.rsqrt(spread + EPSILON)


def split_heads(packed, head_count):
    pieces = jnp.split(packed, 4, axis=-1)
    return [
        piece.reshape(piece.shape[:-1] + (head_count, piece.shape[-1] // head_count))
        for piece in pieces
    ]


def attend(queries, key_rows, value_rows, gate_rows, pair_bias):
    head_size = queries.shape[-1]
    scores = jnp.einsum(
        "bihd,bjhd->bhij", queries, key_rows, preferred_element_type=jnp.float32
    ) / math.sqrt(head_size)
    scores = scores + pair_bias
    highest = jnp.max(scores, axis=-1, keepdims=True)
    expo = jnp.exp(scores - highest)
    weights = (expo / jnp.sum(expo, axis=-1, keepdims=True)).astype(jnp.bfloat16)
    attended = jnp.einsum(
        "bhij,bjhd->bihd", weights, value_rows, preferred_element_type=jnp.float32
    )
    gated = (jax.nn.sigmoid(gate_rows.astype(jnp.float32)) * attended).astype(jnp.bfloat16)
    return gated.reshape(gated.shape[:2] + (gated.shape[2] * gated.shape[3],))


def mapped_horizontal_piece(homolog_features, horizontal_attend_entry_maps):
    horizontal_standardized = standardize_features(homolog_features).astype(jnp.bfloat16)
    return jnp.einsum(
        "src,cf->srf",
        horizontal_standardized,
        horizontal_attend_entry_maps,
        preferred_element_type=jnp.float32,
    ).astype(jnp.bfloat16)


def collect_bias(twofold_features, twofold_offset_map):
    pair_norm = standardize_features(twofold_features).astype(jnp.bfloat16)
    local_bias = jnp.einsum(
        "ijz,zh->hij", pair_norm, twofold_offset_map, preferred_element_type=jnp.float32
    ).astype(jnp.bfloat16)
    return lax.all_gather(local_bias, "dap", axis=1, tiled=True)


def column_delta(received_blocks, vertical_attend_entry_maps, vertical_attend_exit_map, head_count):
    column_alignment = received_blocks[:, 0]
    column_layer_norm = standardize_features(column_alignment).astype(jnp.bfloat16)
    col_proj = jnp.einsum(
        "skc,cf->ksf",
        column_layer_norm,
        vertical_attend_entry_maps,
        preferred_element_type=jnp.float32,
    ).astype(jnp.bfloat16)
    queries, key_rows, value_rows, gate_rows = split_heads(col_proj, head_count)
    column_gated_output = attend(queries, key_rows, value_rows, gate_rows, 0.0)
    residual_delta = jnp.einsum(
        "ksf,fc->skc",
        column_gated_output,
        vertical_attend_exit_map,
        preferred_element_type=jnp.float32,
    )
    return (column_alignment.astype(jnp.float32) + residual_delta).astype(jnp.bfloat16)


def per_device(
    homolog_features,
    twofold_features,
    twofold_offset_map,
    horizontal_attend_entry_maps,
    horizontal_attend_exit_map,
    vertical_attend_entry_maps,
    vertical_attend_exit_map,
    tensor_product_factors,
    tensor_product_exit_map,
):
    head_count = twofold_offset_map.shape[1]
    horizontal_mapped_features = mapped_horizontal_piece(
        homolog_features, horizontal_attend_entry_maps
    )
    gathered = collect_bias(twofold_features, twofold_offset_map)
    bias_wide = gathered.astype(jnp.float32)[None]
    heads_row = split_heads(horizontal_mapped_features, head_count)

    def one_sequence(items):
        return attend(items[0][None], items[1][None], items[2][None], items[3][None], bias_wide)[0]

    horizontal_sigmoid_scaled = lax.map(one_sequence, tuple(heads_row))
    homolog_line = (
        homolog_features.astype(jnp.float32)
        + jnp.einsum(
            "asd,dy->asy",
            horizontal_sigmoid_scaled,
            horizontal_attend_exit_map,
            preferred_element_type=jnp.float32,
        )
    ).astype(jnp.bfloat16)
    parallel_width = lax.axis_size("dap")
    sequence_local, residue_total, channel_count = homolog_line.shape
    alignment_blocks = homolog_line.reshape(
        sequence_local, parallel_width, residue_total // parallel_width, channel_count
    )
    alignment_output = column_delta(
        lax.all_to_all(alignment_blocks, "dap", split_axis=1, concat_axis=0, tiled=True),
        vertical_attend_entry_maps,
        vertical_attend_exit_map,
        head_count,
    )
    outer_width = tensor_product_factors.shape[1] // 2
    homolog_tally = alignment_output.shape[0]
    residue_local = alignment_output.shape[1]
    outer_layer_norm = standardize_features(alignment_output).astype(jnp.bfloat16)
    left_rows = jnp.einsum(
        "src,cf->rsf",
        outer_layer_norm,
        tensor_product_factors[:, :outer_width],
        preferred_element_type=jnp.float32,
    ).astype(jnp.bfloat16)
    right_rows = jnp.einsum(
        "src,cf->rsf",
        outer_layer_norm,
        tensor_product_factors[:, outer_width:],
        preferred_element_type=jnp.float32,
    ).astype(jnp.bfloat16)
    right_flat = right_rows.reshape(residue_local, homolog_tally * outer_width)
    segment = lax.all_gather(right_flat, "dap", axis=0, tiled=True)
    count_rows = segment.shape[0]
    right_three = segment.reshape(count_rows, homolog_tally, outer_width)
    product = (
        jnp.einsum("isc,jse->ijce", left_rows, right_three, preferred_element_type=jnp.float32)
        / homolog_tally
    )
    flat = product.astype(jnp.bfloat16).reshape(
        residue_local * count_rows, outer_width * outer_width
    )
    residual_delta = jnp.dot(flat, tensor_product_exit_map, preferred_element_type=jnp.float32)
    residual_delta = residual_delta.reshape(residue_local, count_rows, residual_delta.shape[-1])
    base_rows = twofold_features.astype(jnp.float32)
    pair_output = (base_rows + residual_delta).astype(jnp.bfloat16)
    return (alignment_output, pair_output)


def solution(mesh):
    in_specs = (
        P(("crop", "dap"), None, None),
        P(("crop", "dap"), None, None),
        P(),
        P(),
        P(),
        P(),
        P(),
        P(),
        P(),
    )
    out_specs = (P("crop", "dap", None), P(("crop", "dap"), None, None))
    return jax.shard_map(
        per_device, mesh=mesh, in_specs=in_specs, out_specs=out_specs, check_vma=False
    )
```

profile of v0, /device:TPU:0, one launch (start us, length us, event | category | flops | bytes accessed | tf_op | source)
XLA Modules:
  0.0 153.7 jit_solution(9199127318719284035)
XLA Ops:
  7.2 0.0 all-gather.3.cloned.1.call-start
  7.2 1.1 convert_reduce_fusion
  8.4 1.2 fusion.38
  9.6 1.4 convolution_convert_fusion.1
  11.1 0.1 fusion.80
  11.2 0.2 copy.76
  11.4 0.2 copy.77
  11.5 0.2 copy.74
  11.7 0.2 copy.75
  11.9 0.1 copy-done.2
  12.0 0.1 convert_reduce_fusion.2
  12.1 0.2 fusion.48
  12.4 0.3 fusion.32
  12.7 43.9 %all_gather.6 = bf16[8,128,128]{2,0,1:T(8,128)(2,1)S(1)} all-gather(bf16[8,4,128]{2,0,1:T(8,128)(2,1)S(1)} %fusion.32), channel_id=1, replica_groups=mesh['crop'=1,'dap'=32] {'dap'}, dimensions={1}, use_global_device_ids=true | all-gather | bytes 270336 | tf_op jit(solution)/shard_map/all_gather | solution.py:56
  56.6 0.2 copy.78
  56.9 3.8 %while.10 = (s32[]{:T(128)}, bf16[4,128,256]{1,2,0:T(8,128)(2,1)S(1)}, bf16[4,128,8,32]{1,3,2,0:T(8,128)(2,1)S(1)}, bf16[4,128,8,32]{1,3,2,0:T(8,128)(2,1)S(1)},...) while((s32[]{:T(128)}, ...), condition=%wide.region_7.8_spmd, body=%wide.region_4.7_spmd.sunk | while | flops 26543360 | bytes 3222617 | solution.py:101
  56.9 0.3 fusion.106
  57.2 0.4 fusion.105
  57.6 0.2 fusion.107
  57.9 0.3 fusion.106
  58.2 0.4 fusion.105
  58.5 0.2 fusion.107
  58.8 0.3 fusion.106
  59.1 0.4 fusion.105
  59.5 0.2 fusion.107
  59.8 0.3 fusion.106
  60.1 0.4 fusion.105
  60.4 0.2 fusion.107
  60.7 0.3 fusion.27
  61.0 0.1 reshape.159
  61.1 0.1 copy.80
  61.2 12.3 %all_to_all.4 = bf16[4,32,4,256]{3,2,0,1:T(4,128)(2,1)S(1)} all-to-all(bf16[4,32,4,256]{3,2,0,1:T(4,128)(2,1)S(1)} %copy.80), channel_id=1, replica_groups=mesh['crop'=1,'dap'=32] {'dap'}, dimensions={1} | all-to-all | bytes 524288 | tf_op jit(solution)/shard_map/all_to_all | solution.py:117
  73.5 0.3 bitcast_reduce_fusion
  73.8 0.1 copy.83
  73.9 0.1 copy.85
  74.0 0.1 copy.84
  74.1 0.5 fusion.44
  74.6 0.1 copy.87
  74.7 0.1 copy.88
  74.8 0.1 rsqrt.38
  74.9 0.1 div.69
  75.0 0.1 bitcast_convert_fusion.1
  75.2 0.5 fusion.22
  75.7 0.1 fusion.79
  75.7 0.1 add_divide_fusion
  75.9 0.2 copy.91
  76.1 0.2 copy.92
  76.3 0.2 copy.90
  76.4 0.2 copy.89
  76.6 2.2 %fusion.81 = (f32[4,8,128]{2,1,0:T(8,128)S(1)}, f32[4,8,128,128]{2,3,1,0:T(8,128)}) fusion(bf16[4,128,8,32]{1,3,2,0:T(8,128)(2,1)S(1)} %bitcast.155, bf16[4,128,8,32]{1,3,2,0:T(8,128)(2,1)S(1)} %bitcast.156), kind=kOutput, calls=%fused_computation.102 | convolution fusion | flops 35127424 | bytes 2637824 | tf_op jit(solution)/shard_map/sub | solution.py:32
  78.9 2.0 %fusion.26 = bf16[4,128,8,32]{1,3,2,0:T(8,128)(2,1)S(1)} fusion(f32[4,128,8,32]{1,3,2,0:T(8,128)S(1)} %bitcast.152, bf16[4,128,8,32]{1,3,2,0:T(8,128)(2,1)S(1)} %bitcast.157, f32[4,8,128,128]{2,3,1,0:T(8,128)} %get-tuple-element.98, f32[4,8,128]{2,1,0:T(8,128)S(1)} %get-tuple-element.97), kind=kOutput, calls=%fused_computation.35 | convolution fusion | flops 34865152 | bytes 3162112 | tf_op jit(solution)/shard_map/bhij,bjhd->bihd/dot_general | solution.py:34
  80.9 0.4 convert_reduce_fusion.1
  81.3 0.2 fusion.40
  81.6 0.3 fusion.30
  81.9 0.1 copy.95
  82.0 0.8 reshape.172
  82.8 0.0 all-gather.3.cloned.1.call-update
  82.9 0.9 copy.99
  83.8 50.6 %all-gather.3.cloned.1.call-done = bf16[32,4,4096]{2,1,0:T(4,128)(2,1)} async-done(((bf16[1,4,4096]{2,1,0:T(4,128)(2,1)}), bf16[32,4,4096]{2,1,0:T(4,128)(2,1)}) %all-gather.3.cloned.1.call-update) | async-done | bytes 1048592 | tf_op jit(solution)/shard_map/all_gather | solution.py:139
  134.3 5.9 %reshape.165 = bf16[128,128,32]{2,1,0:T(8,128)(2,1)} reshape(bf16[32,4,4096]{2,1,0:T(4,128)(2,1)} %all-gather.3.cloned.1.call-done) | data formatting | bytes 2097152 | tf_op jit(solution)/shard_map/reshape | solution.py:141
  140.2 4.0 %copy.104 = bf16[128,128,32,1]{1,0,3,2:T(8,128)(2,1)S(1)} copy(bf16[128,128,32,1]{2,1,0,3:T(8,128)(2,1)} %bitcast.145) | data formatting | bytes 2097152 | tf_op jit(solution)/shard_map/reshape | solution.py:141
  144.2 0.7 fusion.23
  145.0 0.7 copy.97
  145.7 1.1 fusion.29
  (31 shorter events, 0.2 us)
Async XLA Ops:
  7.2 2.4 %copy-start = (bf16[256,1024]{1,0:T(8,128)(2,1)S(1)}, bf16[256,1024]{1,0:T(8,128)(2,1)}, u32[]{:S(2)}) copy-start(bf16[256,1024]{1,0:T(8,128)(2,1)} %param.14) | copy-start | bytes 1572868
  7.2 127.2 %all-gather.3.cloned.1.call-start = ((), (), s32[]{:S(2)}) async-start(), calls=%async_computation.1 | async-start | bytes 1081344 | tf_op jit(solution)/shard_map/all_gather | solution.py:139
  11.1 0.9 copy-start.2
  11.1 1.3 copy-start.8
  56.9 3.8 %copy-start.1 = (bf16[4,128,256]{2,1,0:T(8,128)(2,1)S(1)}, bf16[4,128,256]{2,1,0:T(8,128)(2,1)}, u32[]{:S(2)}) copy-start(bf16[4,128,256]{2,1,0:T(8,128)(2,1)} %param.11) | copy-start | bytes 786436
  56.9 3.8 %copy-start.5 = (bf16[256,256]{1,0:T(8,128)(2,1)S(1)}, bf16[256,256]{1,0:T(8,128)(2,1)}, u32[]{:S(2)}) copy-start(bf16[256,256]{1,0:T(8,128)(2,1)} %param.15) | copy-start | bytes 393220
  60.7 14.4 %copy-start.3 = (bf16[256,1024]{1,0:T(8,128)(2,1)S(1)}, bf16[256,1024]{1,0:T(8,128)(2,1)}, u32[]{:S(2)}) copy-start(bf16[256,1024]{1,0:T(8,128)(2,1)} %param.16) | copy-start | bytes 1572868
  78.9 2.0 %copy-start.6 = (bf16[256,256]{1,0:T(8,128)(2,1)S(1)}, bf16[256,256]{1,0:T(8,128)(2,1)}, u32[]{:S(2)}) copy-start(bf16[256,256]{1,0:T(8,128)(2,1)} %param.17) | copy-start | bytes 393220
  78.9 2.7 %copy-start.7 = (bf16[256,64]{0,1:T(8,128)(2,1)S(1)}, bf16[256,64]{0,1:T(8,128)(2,1)}, u32[]{:S(2)}) copy-start(bf16[256,64]{0,1:T(8,128)(2,1)} %param.18) | copy-start | bytes 98308
  144.2 1.4 copy-start.4
Sparse Core Ops, SparseCore 0:
  83.0 51.2 all-gather.2
where the time goes:
time: 154 us
  blocking collectives  56.2 us (36%)
  waiting for transfers between devices  50.6 us (33%)
  local copies, waits for them, and re-layouts  15.3 us (10%)
  between operations  14.4 us (9%)
  matrix products  13 us (8%)
  other arithmetic  4.06 us (3%)
    all_gather x1, waiting for transfers between devices, per_device(): segment = lax.all_gather(right_flat, 'dap', axis=0, tiled=True)  50.6 us
    all_gather x1, blocking collectives, collect_bias(): return lax.all_gather(local_bias, 'dap', axis=1, tiled=True)  43.9 us
    all_to_all x1, blocking collectives, per_device(): lax.all_to_all(alignment_blocks, 'dap', split_axis=1, concat_axis=0, tile...  12.3 us
    reshape x2, local copies, waits for them, and re-layouts, per_device(): right_three = segment.reshape(count_rows, homolog_tally, outer_width)  9.9 us
    sub x5, matrix products, attend(): expo = jnp.exp(scores - highest)  3.74 us
  transfers between devices with their start and end apart: 1, of which 1 were waited for; matrix products, arithmetic and copies ran while one was open for 1% of the time, Pallas kernels for 0%

commit v1 on v0

--- a/solution.py
+++ b/solution.py
@@ -53,7 +53,7 @@
     local_bias = jnp.einsum(
         "ijz,zh->hij", pair_norm, twofold_offset_map, preferred_element_type=jnp.float32
     ).astype(jnp.bfloat16)
-    return lax.all_gather(local_bias, "dap", axis=1, tiled=True)
+    return jnp.concatenate(lax.all_gather(local_bias, "dap"), axis=1)
 
 
 def column_delta(received_blocks, vertical_attend_entry_maps, vertical_attend_exit_map, head_count):

time: 154 us -> 154 us (level)
  no operation moved by 1% of the time
where the time goes in v1:
time: 154 us
  blocking collectives  56.2 us (36%)
  waiting for transfers between devices  50.6 us (33%)
  local copies, waits for them, and re-layouts  15.3 us (10%)
  between operations  14.4 us (9%)
  matrix products  13 us (8%)
  other arithmetic  4.06 us (3%)
    all_gather x1, waiting for transfers between devices, per_device(): segment = lax.all_gather(right_flat, 'dap', axis=0, tiled=True)  50.6 us
    all_gather x1, blocking collectives, collect_bias(): return jnp.concatenate(lax.all_gather(local_bias, 'dap'), axis=1)  43.9 us
    all_to_all x1, blocking collectives, per_device(): lax.all_to_all(alignment_blocks, 'dap', split_axis=1, concat_axis=0, tile...  12.3 us
    reshape x2, local copies, waits for them, and re-layouts, per_device(): right_three = segment.reshape(count_rows, homolog_tally, outer_width)  9.9 us
    sub x5, matrix products, attend(): expo = jnp.exp(scores - highest)  3.74 us
  transfers between devices with their start and end apart: 1, of which 1 were waited for; matrix products, arithmetic and copies ran while one was open for 1% of the time, Pallas kernels for 0%

profile of v1, /device:TPU:0, one launch (start us, length us, event | category | flops | bytes accessed | tf_op | source)
XLA Modules:
  0.0 153.7 jit_solution(8265886534573709663)
XLA Ops:
  7.2 0.0 all-gather.4.cloned.1.call-start
  7.2 1.1 convert_reduce_fusion
  8.4 1.2 fusion.38
  9.6 1.4 convolution_convert_fusion.1
  11.1 0.1 fusion.80
  11.2 0.2 copy.78
  11.4 0.2 copy.79
  11.5 0.2 copy.76
  11.7 0.2 copy.77
  11.9 0.1 copy-done.2
  12.0 0.1 convert_reduce_fusion.2
  12.1 0.2 fusion.48
  12.4 0.3 fusion.32
  12.7 43.9 %all-gather = bf16[256,4,128]{2,0,1:T(8,128)(2,1)S(1)} all-gather(bf16[8,4,128]{2,0,1:T(8,128)(2,1)S(1)} %fusion.32), channel_id=2, replica_groups=mesh['crop'=1,'dap'=32] {'dap'}, dimensions={0}, use_global_device_ids=true | all-gather | bytes 270336 | tf_op jit(solution)/shard_map/all_gather | solution.py:56
  56.6 0.1 copy.80
  56.7 0.2 copy.81
  57.0 3.8 %while.10 = (s32[]{:T(128)}, bf16[4,128,256]{1,2,0:T(8,128)(2,1)S(1)}, bf16[4,128,8,32]{1,3,2,0:T(8,128)(2,1)S(1)}, bf16[4,128,8,32]{1,3,2,0:T(8,128)(2,1)S(1)},...) while((s32[]{:T(128)}, ...), condition=%wide.region_7.8_spmd, body=%wide.region_4.7_spmd.sunk | while | flops 26543360 | bytes 3222617 | solution.py:101
  57.0 0.3 fusion.106
  57.3 0.4 fusion.105
  57.7 0.2 fusion.107
  57.9 0.3 fusion.106
  58.2 0.4 fusion.105
  58.6 0.2 fusion.107
  58.9 0.3 fusion.106
  59.2 0.4 fusion.105
  59.6 0.2 fusion.107
  59.8 0.3 fusion.106
  60.1 0.4 fusion.105
  60.5 0.2 fusion.107
  60.8 0.3 fusion.27
  61.1 0.1 reshape.173
  61.2 0.1 copy.83
  61.3 12.3 %all_to_all.4 = bf16[4,32,4,256]{3,2,0,1:T(4,128)(2,1)S(1)} all-to-all(bf16[4,32,4,256]{3,2,0,1:T(4,128)(2,1)S(1)} %copy.83), channel_id=1, replica_groups=mesh['crop'=1,'dap'=32] {'dap'}, dimensions={1} | all-to-all | bytes 524288 | tf_op jit(solution)/shard_map/all_to_all | solution.py:117
  73.6 0.3 bitcast_reduce_fusion
  73.8 0.1 copy.86
  73.9 0.1 copy.88
  74.1 0.1 copy.87
  74.2 0.5 fusion.44
  74.6 0.1 copy.90
  74.7 0.1 copy.91
  74.9 0.1 rsqrt.38
  75.0 0.1 div.69
  75.1 0.1 bitcast_convert_fusion.1
  75.2 0.5 fusion.22
  75.7 0.1 fusion.79
  75.8 0.1 add_divide_fusion
  76.0 0.2 copy.94
  76.1 0.2 copy.95
  76.3 0.2 copy.93
  76.5 0.2 copy.92
  76.7 2.2 %fusion.81 = (f32[4,8,128]{2,1,0:T(8,128)S(1)}, f32[4,8,128,128]{2,3,1,0:T(8,128)}) fusion(bf16[4,128,8,32]{1,3,2,0:T(8,128)(2,1)S(1)} %bitcast.159, bf16[4,128,8,32]{1,3,2,0:T(8,128)(2,1)S(1)} %bitcast.160), kind=kOutput, calls=%fused_computation.102 | convolution fusion | flops 35127424 | bytes 2637824 | tf_op jit(solution)/shard_map/sub | solution.py:32
  79.0 2.0 %fusion.26 = bf16[4,128,8,32]{1,3,2,0:T(8,128)(2,1)S(1)} fusion(f32[4,128,8,32]{1,3,2,0:T(8,128)S(1)} %bitcast.156, bf16[4,128,8,32]{1,3,2,0:T(8,128)(2,1)S(1)} %bitcast.161, f32[4,8,128,128]{2,3,1,0:T(8,128)} %get-tuple-element.98, f32[4,8,128]{2,1,0:T(8,128)S(1)} %get-tuple-element.97), kind=kOutput, calls=%fused_computation.35 | convolution fusion | flops 34865152 | bytes 3162112 | tf_op jit(solution)/shard_map/bhij,bjhd->bihd/dot_general | solution.py:34
  81.0 0.4 convert_reduce_fusion.1
  81.4 0.2 fusion.40
  81.6 0.3 fusion.30
  82.0 0.1 copy.98
  82.1 0.8 reshape.188
  82.9 0.9 copy.102
  83.8 50.6 %all-gather.4.cloned.1.call-done = bf16[32,4,4096]{2,1,0:T(4,128)(2,1)} async-done(((bf16[1,4,4096]{2,1,0:T(4,128)(2,1)}), bf16[32,4,4096]{2,1,0:T(4,128)(2,1)}) %all-gather.4.cloned.1.call-update) | async-done | bytes 1048592 | tf_op jit(solution)/shard_map/all_gather | solution.py:139
  134.4 5.9 %reshape.179 = bf16[128,128,32]{2,1,0:T(8,128)(2,1)} reshape(bf16[32,4,4096]{2,1,0:T(4,128)(2,1)} %all-gather.4.cloned.1.call-done) | data formatting | bytes 2097152 | tf_op jit(solution)/shard_map/reshape | solution.py:141
  140.3 4.0 %copy.107 = bf16[128,128,32,1]{1,0,3,2:T(8,128)(2,1)S(1)} copy(bf16[128,128,32,1]{2,1,0,3:T(8,128)(2,1)} %bitcast.148) | data formatting | bytes 2097152 | tf_op jit(solution)/shard_map/reshape | solution.py:141
  144.3 0.7 fusion.23
  145.0 0.7 copy.100
  145.7 1.1 fusion.29
  (32 shorter events, 0.2 us)
Async XLA Ops:
  7.2 2.4 %copy-start = (bf16[256,1024]{1,0:T(8,128)(2,1)S(1)}, bf16[256,1024]{1,0:T(8,128)(2,1)}, u32[]{:S(2)}) copy-start(bf16[256,1024]{1,0:T(8,128)(2,1)} %param.14) | copy-start | bytes 1572868
  7.2 127.2 %all-gather.4.cloned.1.call-start = ((), (), s32[]{:S(2)}) async-start(), calls=%async_computation.1 | async-start | bytes 1081344 | tf_op jit(solution)/shard_map/all_gather | solution.py:139
  11.1 0.9 copy-start.2
  11.1 1.3 copy-start.8
  57.0 3.8 %copy-start.1 = (bf16[4,128,256]{2,1,0:T(8,128)(2,1)S(1)}, bf16[4,128,256]{2,1,0:T(8,128)(2,1)}, u32[]{:S(2)}) copy-start(bf16[4,128,256]{2,1,0:T(8,128)(2,1)} %param.11) | copy-start | bytes 786436
  57.0 3.8 %copy-start.5 = (bf16[256,256]{1,0:T(8,128)(2,1)S(1)}, bf16[256,256]{1,0:T(8,128)(2,1)}, u32[]{:S(2)}) copy-start(bf16[256,256]{1,0:T(8,128)(2,1)} %param.15) | copy-start | bytes 393220
  60.8 14.4 %copy-start.3 = (bf16[256,1024]{1,0:T(8,128)(2,1)S(1)}, bf16[256,1024]{1,0:T(8,128)(2,1)}, u32[]{:S(2)}) copy-start(bf16[256,1024]{1,0:T(8,128)(2,1)} %param.16) | copy-start | bytes 1572868
  78.9 2.0 %copy-start.6 = (bf16[256,256]{1,0:T(8,128)(2,1)S(1)}, bf16[256,256]{1,0:T(8,128)(2,1)}, u32[]{:S(2)}) copy-start(bf16[256,256]{1,0:T(8,128)(2,1)} %param.17) | copy-start | bytes 393220
  79.0 2.7 %copy-start.7 = (bf16[256,64]{0,1:T(8,128)(2,1)S(1)}, bf16[256,64]{0,1:T(8,128)(2,1)}, u32[]{:S(2)}) copy-start(bf16[256,64]{0,1:T(8,128)(2,1)} %param.18) | copy-start | bytes 98308
  144.3 1.4 copy-start.4
Sparse Core Ops, SparseCore 0:
  83.1 51.2 all-gather.3
